TPU v7x, 512 devices: a whole 4x8x8 slice. The times are simulated.
512 devices in a mesh: row: 16 (over y_lo, x, core), col: 32 (over y_hi, z).
Axes of the slice: x: 4, y: 8 (y_hi: 4, y_lo: 2; y = y_hi * 2 + y_lo), z: 8, core: 2. Of those that a mesh axis runs over, the one named last changes fastest.
Arguments:
- object_field: float32 [2, 4096, 8192], P(None, 'row', 'col'), may hold values from -6 to 6
- probe: float32 [2, 128, 128], replicated, may hold values from -6 to 6
- amplitude: bfloat16 [16, 32, 16, 128, 128], P('row', 'col'), may hold values from 0 to 2
- corners: int32 [2, 16, 32, 16], P(None, 'row', 'col'), may hold values from 0 to 255, as said below
- live_count: int32 [16, 32], P('row', 'col'), may hold values from 4 to 16, as said below
Outputs:
- refined_object: float32 [2, 4096, 8192], P(None, 'row', 'col')
- new_probe: float32 [2, 128, 128], replicated
Inputs may be any that keep to these rules, and one draw needn't show every extreme that they name: In the last tile row of the mesh corners[0] is at most 128, and in the last tile column corners[1] is at most 128, so every window lies inside the object. Outside the last tile row, corners[0] of slot 0 is at least 192; outside the last tile column, corners[1] of slot 0 is at least 192. Unused slots carry valid corners. Slots from live_count on are unused. Some tile uses all 16 slots in every draw.
All inputs are finite; a program needn't handle non-finite values.
Results may differ from a plain program's by a relative error of at most 0.0039.
The roundings to bfloat16 on the way count: a program that leaves them out, or rounds other values in their place, can miss the bound.
Values may be sent and summed in bfloat16 or wider, within the bound.
No kernel may reach another device: no remote copies, remote signals or barrier semaphores. Data moves between devices by JAX's collectives and lax.ppermute only.
A program may use at most 64 MiB of HBM per device.

v0:
```python
import math
import jax
import jax.numpy as jnp
from jax import lax
from jax.sharding import PartitionSpec as P

BLOCK = 4


def from_behind(value, axis, steps):
    count = lax.axis_size(axis)
    first, last = (max(0, -steps), min(count, count - steps))
    return lax.ppermute(value, axis, [(source, source + steps) for source in range(first, last)])


def dft_tables(window):
    indices = jnp.arange(window, dtype=jnp.int32)
    phase_index = indices[:, None] * indices[None, :] % window
    angles = phase_index.astype(jnp.float32) * (2.0 * math.pi / window)
    norming = 1.0 / math.sqrt(window)
    cosines = jnp.cos(angles) * norming
    sines = jnp.sin(angles) * norming
    forward_fourier = jnp.stack([jnp.stack([cosines, -sines]), jnp.stack([sines, cosines])])
    inverse_fourier = jnp.stack([jnp.stack([cosines, sines]), jnp.stack([-sines, cosines])])
    return (forward_fourier.astype(jnp.bfloat16), inverse_fourier.astype(jnp.bfloat16))


def times(left_value, right_value):
    real_part = (
        left_value[..., 0, :, :] * right_value[..., 0, :, :]
        - left_value[..., 1, :, :] * right_value[..., 1, :, :]
    )
    imag_part = (
        left_value[..., 0, :, :] * right_value[..., 1, :, :]
        + left_value[..., 1, :, :] * right_value[..., 0, :, :]
    )
    return jnp.stack([real_part, imag_part], -3)


def times_conj(left_value, right_value):
    real_part = (
        left_value[..., 0, :, :] * right_value[..., 0, :, :]
        + left_value[..., 1, :, :] * right_value[..., 1, :, :]
    )
    imag_part = (
        left_value[..., 0, :, :] * right_value[..., 1, :, :]
        - left_value[..., 1, :, :] * right_value[..., 0, :, :]
    )
    return jnp.stack([real_part, imag_part], -3)


def refine_object(exit_waves, measured_intensity, forward_fourier, inverse_fourier):
    half_done = jnp.einsum(
        "bcrk,cdkm->bdrm", exit_waves, forward_fourier, preferred_element_type=jnp.float32
    ).astype(jnp.bfloat16)
    spectrum = jnp.einsum(
        "cdrs,bcsm->bdrm", forward_fourier, half_done, preferred_element_type=jnp.float32
    )
    modulus = jnp.sqrt(spectrum[:, 0] * spectrum[:, 0] + spectrum[:, 1] * spectrum[:, 1])
    rescale = measured_intensity.astype(jnp.float32) / jnp.maximum(modulus, 0.5)
    projected = (spectrum * rescale[:, None]).astype(jnp.bfloat16)
    half_back = jnp.einsum(
        "bcrk,cdkm->bdrm", projected, inverse_fourier, preferred_element_type=jnp.float32
    ).astype(jnp.bfloat16)
    returned = jnp.einsum(
        "cdrs,bcsm->bdrm", inverse_fourier, half_back, preferred_element_type=jnp.float32
    )
    return returned - exit_waves.astype(jnp.float32)


def refine_all(exit_waves, measured_intensity, update_marks, forward_fourier, inverse_fourier):
    group_size = BLOCK
    turns = exit_waves.shape[0] // group_size
    collected = jnp.zeros(exit_waves.shape, jnp.float32)

    def advance(position, collected):
        offset = position * group_size
        exit_wave_portion = lax.dynamic_slice_in_dim(exit_waves, offset, group_size, 0)
        measured_part = lax.dynamic_slice_in_dim(measured_intensity, offset, group_size, 0)
        any_used = jnp.any(lax.dynamic_slice_in_dim(update_marks, offset, group_size, 0))
        object_delta = lax.cond(
            any_used,
            lambda exit_wave_current, measurement_current: refine_object(
                exit_wave_current, measurement_current, forward_fourier, inverse_fourier
            ),
            lambda exit_wave_current, measurement_current: jnp.zeros(
                exit_wave_current.shape, jnp.float32
            ),
            exit_wave_portion,
            measured_part,
        )
        return lax.dynamic_update_slice_in_dim(collected, object_delta, offset, 0)

    return lax.fori_loop(0, turns, advance, collected)


def extend(current, window):
    right_rim = from_behind(current[:, :, :window], "col", -1)
    lower_rim = from_behind(current[:, :window, :], "row", -1)
    corner_rim = from_behind(
        current[:, :window, :window], ("row", "col"), -(lax.axis_size("col") + 1)
    )
    widened = jnp.concatenate([current, right_rim], 2)
    lower_wide = jnp.concatenate([lower_rim, corner_rim], 2)
    return jnp.concatenate([widened, lower_wide], 1)


def fold(deposit, window):
    tile_size = deposit.shape[1] - window
    spilled = from_behind(deposit[:, tile_size:, :tile_size], "row", 1)
    right_part = from_behind(deposit[:, :tile_size, tile_size:], "col", 1)
    corner_part = from_behind(
        deposit[:, tile_size:, tile_size:], ("row", "col"), lax.axis_size("col") + 1
    )
    result = deposit[:, :tile_size, :tile_size]
    result = result.at[:, :window, :].add(spilled)
    result = result.at[:, :, :window].add(right_part)
    return result.at[:, :window, :window].add(corner_part)


def sweep(
    current,
    probe,
    work_measured,
    used,
    work_used,
    corner_list,
    forward_fourier,
    inverse_fourier,
    with_light,
):
    window = probe.shape[1]
    tile_size = current.shape[1]
    slots = used.shape[0]
    extended = extend(current, window)
    zero_index = jnp.zeros((), jnp.int32)

    def cut_patch(spot):
        return lax.dynamic_slice(extended, (zero_index, spot[0], spot[1]), (2, window, window))

    patches = jax.vmap(cut_patch)(corner_list)
    exit_waves = times(probe[None], patches).astype(jnp.bfloat16)
    object_delta = refine_all(
        exit_waves, work_measured, work_used, forward_fourier, inverse_fourier
    )
    weights = used.astype(jnp.float32)
    object_delta = object_delta * weights[:, None, None, None]
    pushed = times_conj(probe[None], object_delta)
    if with_light:
        power = probe[0] * probe[0] + probe[1] * probe[1]
        lighting = power[None] * weights[:, None, None]
        pushed = jnp.concatenate([pushed, lighting[:, None]], 1)
    channels = pushed.shape[1]
    deposit = jnp.zeros((channels, tile_size + window, tile_size + window), jnp.float32)

    def place(position, deposit):
        spot = corner_list[position]
        anchor = (zero_index, spot[0], spot[1])
        present = lax.dynamic_slice(deposit, anchor, (channels, window, window))
        return lax.dynamic_update_slice(deposit, present + pushed[position], anchor)

    deposit = lax.fori_loop(0, slots, place, deposit)
    gathered = fold(deposit, window)
    gradient = None
    if not with_light:
        gradient = jnp.sum(times_conj(patches, object_delta), 0)
    return (gathered, gradient)


def on_device(object_field, probe, amplitude, corners, live_count):
    slots = amplitude.shape[2]
    window = probe.shape[1]
    measured_intensity = amplitude.reshape(slots, window, window)
    corner_list = jnp.transpose(corners.reshape(2, slots))
    used = jnp.arange(slots, dtype=jnp.int32) < live_count.reshape(())
    forward_fourier, inverse_fourier = dft_tables(window)
    first_pass, unused_grad = sweep(
        object_field,
        probe,
        measured_intensity,
        used,
        used,
        corner_list,
        forward_fourier,
        inverse_fourier,
        True,
    )
    denominator = first_pass[2] + 4.0
    updated = object_field + first_pass[:2] / denominator
    second_pass, gradient = sweep(
        updated,
        probe,
        measured_intensity,
        used,
        used,
        corner_list,
        forward_fourier,
        inverse_fourier,
        False,
    )
    refined_object = updated + second_pass / denominator
    summed = lax.psum(gradient, ("row", "col"))
    spread = jnp.sqrt(jnp.mean(summed[0] * summed[0] + summed[1] * summed[1]) + 1e-06)
    new_probe = probe + summed / spread
    return (refined_object, new_probe)


def solution(mesh):
    in_specs = (
        P(None, "row", "col"),
        P(),
        P("row", "col", None, None, None),
        P(None, "row", "col", None),
        P("row", "col"),
    )
    out_specs = (P(None, "row", "col"), P())
    return jax.shard_map(
        on_device, mesh=mesh, in_specs=in_specs, out_specs=out_specs, check_vma=False
    )
```

profile of v0, /device:TPU:1, one launch (start us, length us, event | category | flops | bytes accessed | tf_op | source)
XLA Modules:
  0.0 658.6 jit_solution(6017470516622135121)
XLA Ops:
  10.5 8.9 %collective-permute-start.1 = (f32[2,128,256]{2,1,0:T(8,128)S(1)}, f32[2,128,256]{2,1,0:T(8,128)S(1)}, u32[]{:S(2)}, u32[]{:S(2)}) collective-permute-start(f32[2,128,256]{2,1,0:T(8,128)S(1)} %slice.346), channel_id=1, source_target_pairs={{32,0},{64,32},{96,64},{128,96},{160,128},{192,160},{224,192},{256... | collective-permute-start | bytes 786440 | tf_op jit(solution)/shard_map/ppermute | solution.py:13
  28.9 49.5 %while.64 = (s32[]{:T(128)}, f32[2,384,384]{2,1,0:T(8,128)}, s32[16,3]{0,1:T(4,128)S(1)}, f32[16,2,128,128]{3,2,1,0:T(8,128)S(1)}, s32[]{:T(128)}) while((s32[]{:T(128)}, f32[2,384,384]{2,1,0:T(8,128)}, s32[16,3]{0,1:T(4,128)S(1)}, f32[16,2,128,128]{3,2,1,0:T(8,128)S(1)}, s32[]{:T(128)}) %tuple.206), condition=%wide.while_cond.6, body=%wide.while_body.6.sunk | while | flops 2 | bytes 262261 | solution.py:139
  29.6 2.4 bitcast_dynamic-update-slice_fusion.4
  32.7 2.4 bitcast_dynamic-update-slice_fusion.4
  35.8 2.4 bitcast_dynamic-update-slice_fusion.4
  38.8 2.4 bitcast_dynamic-update-slice_fusion.4
  41.9 2.4 bitcast_dynamic-update-slice_fusion.4
  45.0 2.4 bitcast_dynamic-update-slice_fusion.4
  48.1 2.4 bitcast_dynamic-update-slice_fusion.4
  51.2 2.4 bitcast_dynamic-update-slice_fusion.4
  54.3 2.4 bitcast_dynamic-update-slice_fusion.4
  57.4 2.4 bitcast_dynamic-update-slice_fusion.4
  60.5 2.4 bitcast_dynamic-update-slice_fusion.4
  63.6 2.4 bitcast_dynamic-update-slice_fusion.4
  66.7 2.4 bitcast_dynamic-update-slice_fusion.4
  69.8 2.4 bitcast_dynamic-update-slice_fusion.4
  72.9 2.4 bitcast_dynamic-update-slice_fusion.4
  76.0 2.4 bitcast_dynamic-update-slice_fusion.4
  81.0 12.3 %while.60 = (s32[]{:T(128)}, f32[16,2,128,128]{3,2,1,0:T(8,128)}, pred[16]{0:T(512)(128)(4,1)S(1)}, bf16[16,2,128,128]{2,3,1,0:T(8,128)(2,1)S(1)}, bf16[2,2,128,...) while((s32[]{:T(128)}, f32[16,2,128,128]{3,2,1,0:T(8,128)}, ...), condition=%wide.region_4.5_spmd, body=%wide.region_0.4_spmd.sunk | while | flops 269615104 | bytes 5898981 | solution.py:94
  98.6 137.3 %while.61 = (s32[]{:T(128)}, f32[3,384,384]{2,1,0:T(8,128)S(1)}, s32[16,2]{0,1:T(2,128)S(1)}, f32[16,3,128,128]{3,2,1,0:T(8,128)}, s32[]{:T(128)}, /*index=5*/s32[]{:T(128)}, s32[]{:T(128)}) while((s32[]{:T(128)}, f32[3,384,384]{2,1,0:T(8,128)S(1)}, s32[16,2]{0,1:T(2,128)S(1)}, f32[16,3,128,128]{3,2,1,0:T(8,128)}, s32[]{:T(128)}, ...), condition=%wide.region_6.7_spmd, body=%wide.region_5.6_spmd.sunk | while | flops 49160 | bytes 983237 | solution.py:162
  104.3 2.7 dynamic_update_slice.35
  112.7 3.1 dynamic_update_slice.35
  129.0 3.1 dynamic_update_slice.35
  137.7 3.1 dynamic_update_slice.35
  146.4 3.1 dynamic_update_slice.35
  155.2 2.9 dynamic_update_slice.35
  163.7 2.8 dynamic_update_slice.35
  172.2 3.0 dynamic_update_slice.35
  180.9 2.9 dynamic_update_slice.35
  189.4 3.1 dynamic_update_slice.35
  198.2 2.7 dynamic_update_slice.35
  206.6 3.1 dynamic_update_slice.35
  215.3 3.0 dynamic_update_slice.35
  224.1 3.1 dynamic_update_slice.35
  232.8 3.1 dynamic_update_slice.35
  235.9 11.9 %collective-permute-start.3 = (f32[3,128,256]{2,1,0:T(8,128)S(1)}, f32[3,128,256]{2,1,0:T(8,128)S(1)}, u32[]{:S(2)}, u32[]{:S(2)}) collective-permute-start(f32[3,128,256]{2,1,0:T(8,128)S(1)} %slice.359), channel_id=1, source_target_pairs={{0,32},{32,64},{64,96},{96,128},{128,160},{160,192},{192,224},{224... | collective-permute-start | bytes 1179656 | tf_op jit(solution)/shard_map/ppermute | solution.py:13
  252.6 5.2 collective-permute-done.4
  264.6 16.0 %collective-permute-done.8 = f32[2,128,128]{2,1,0:T(8,128)S(1)} collective-permute-done((f32[2,128,128]{2,1,0:T(8,128)S(1)}, f32[2,128,128]{2,1,0:T(8,128)S(1)}, u32[]{:S(2)}, u32[]{:S(2)}) %collective-permute-start.8) | collective-permute-done | bytes 131104 | tf_op jit(solution)/shard_map/ppermute | solution.py:13
  282.0 49.1 %while.65 = (s32[]{:T(128)}, f32[2,384,384]{2,1,0:T(8,128)}, s32[16,3]{0,1:T(4,128)S(1)}, f32[16,2,128,128]{3,2,1,0:T(8,128)S(1)}, s32[]{:T(128)}) while((s32[]{:T(128)}, f32[2,384,384]{2,1,0:T(8,128)}, s32[16,3]{0,1:T(4,128)S(1)}, f32[16,2,128,128]{3,2,1,0:T(8,128)S(1)}, s32[]{:T(128)}) %tuple.235), condition=%wide.while_cond.7, body=%wide.while_body.7.sunk | while | flops 2 | bytes 262261 | solution.py:139
  282.7 2.4 bitcast_dynamic-update-slice_fusion.5
  285.7 2.4 bitcast_dynamic-update-slice_fusion.5
  291.9 2.4 bitcast_dynamic-update-slice_fusion.5
  298.0 2.4 bitcast_dynamic-update-slice_fusion.5
  304.1 2.4 bitcast_dynamic-update-slice_fusion.5
  307.2 2.4 bitcast_dynamic-update-slice_fusion.5
  313.3 2.4 bitcast_dynamic-update-slice_fusion.5
  319.5 2.4 bitcast_dynamic-update-slice_fusion.5
  322.5 2.4 bitcast_dynamic-update-slice_fusion.5
  325.6 2.4 bitcast_dynamic-update-slice_fusion.5
  328.7 2.4 bitcast_dynamic-update-slice_fusion.5
  336.6 13.6 %while.62 = (s32[]{:T(128)}, f32[16,2,128,128]{3,2,1,0:T(8,128)}, pred[16]{0:T(512)(128)(4,1)S(1)}, bf16[16,2,128,128]{2,3,1,0:T(8,128)(2,1)S(1)}, bf16[2,2,128,...) while((s32[]{:T(128)}, f32[16,2,128,128]{3,2,1,0:T(8,128)}, ...), condition=%wide.region_11.12_spmd, body=%wide.region_7.11_spmd.sunk | while | flops 269615104 | bytes 5898981 | solution.py:94
  355.6 125.7 %while.63 = (s32[]{:T(128)}, f32[2,384,384]{2,1,0:T(8,128)S(1)}, s32[16,2]{0,1:T(2,128)S(1)}, f32[16,2,128,128]{3,2,1,0:T(8,128)}, s32[]{:T(128)}, /*index=5*/s32[]{:T(128)}, s32[]{:T(128)}) while((s32[]{:T(128)}, f32[2,384,384]{2,1,0:T(8,128)S(1)}, s32[16,2]{0,1:T(2,128)S(1)}, f32[16,2,128,128]{3,2,1,0:T(8,128)}, s32[]{:T(128)}, ...), condition=%wide.region_13.14_spmd, body=%wide.region_12.13_spmd.sunk | while | flops 32776 | bytes 655557 | solution.py:162
  368.7 2.5 dynamic_update_slice.37
  383.9 2.5 dynamic_update_slice.37
  391.9 2.5 dynamic_update_slice.37
  399.9 2.5 dynamic_update_slice.37
  423.4 2.4 dynamic_update_slice.37
  439.2 2.5 dynamic_update_slice.37
  454.8 2.5 dynamic_update_slice.37
  462.8 2.5 dynamic_update_slice.37
  470.8 2.5 dynamic_update_slice.37
  478.8 2.5 dynamic_update_slice.37
  482.2 7.6 %collective-permute-start.9 = (f32[2,128,256]{2,1,0:T(8,128)}, f32[2,128,256]{2,1,0:T(8,128)S(1)}, u32[]{:S(2)}, u32[]{:S(2)}) collective-permute-start(f32[2,128,256]{2,1,0:T(8,128)} %slice.375), channel_id=1, source_target_pairs={{0,32},{32,64},{64,96},{96,128},{128,160},{160,192},{192,224},{224... | collective-permute-start | bytes 786440 | tf_op jit(solution)/shard_map/ppermute | solution.py:13
  493.0 153.0 %all-reduce.2.cloned.1.call-done = f32[2,128,128]{2,1,0:T(8,128)} async-done(((f32[2,128,128]{2,1,0:T(8,128)}), f32[2,128,128]{2,1,0:T(8,128)}) %all-reduce.2.cloned.1.call-update) | async-done | bytes 131088 | tf_op jit(solution)/shard_map/psum | solution.py:202
  (321 shorter events, 181.3 us)
Async XLA Ops:
  7.2 19.4 %copy-start.8 = (bf16[1,1,16,128,128]{4,3,2,1,0:T(8,128)(2,1)S(1)}, bf16[1,1,16,128,128]{4,3,2,1,0:T(8,128)(2,1)}, u32[]{:S(2)}) copy-start(bf16[1,1,16,128,128]{4,3,2,1,0:T(8,128)(2,1)} %param.31) | copy-start | bytes 1572868
  7.2 638.8 %all-reduce.2.cloned.1.call-start = ((), (), s32[]{:S(2)}) async-start(), calls=%async_computation | async-start | bytes 262144 | tf_op jit(solution)/shard_map/psum | solution.py:202
  8.2 19.3 %collective-permute-start = (f32[2,256,128]{2,1,0:T(8,128)S(1)}, f32[2,256,128]{2,1,0:T(8,128)S(1)}, u32[]{:S(2)}, u32[]{:S(2)}) collective-permute-start(f32[2,256,128]{2,1,0:T(8,128)S(1)} %slice.345), channel_id=1, source_target_pairs={{1,0},{2,1},{3,2},{4,3},{5,4},{6,5},{7,6},{8,7},{9,8},{10,9},{11,1... | collective-permute-start | bytes 786440 | tf_op jit(solution)/shard_map/ppermute | solution.py:13
  10.5 17.0 %copy-start.4 = (f32[2,256,256]{2,1,0:T(8,128)S(1)}, f32[2,256,256]{2,1,0:T(8,128)}, u32[]{:S(2)}) copy-start(f32[2,256,256]{2,1,0:T(8,128)} %param.29) | copy-start | bytes 1572868
  10.5 17.0 %collective-permute-start.1 = (f32[2,128,256]{2,1,0:T(8,128)S(1)}, f32[2,128,256]{2,1,0:T(8,128)S(1)}, u32[]{:S(2)}, u32[]{:S(2)}) collective-permute-start(f32[2,128,256]{2,1,0:T(8,128)S(1)} %slice.346), channel_id=1, source_target_pairs={{32,0},{64,32},{96,64},{128,96},{160,128},{192,160},{224,192},{256... | collective-permute-start | bytes 786440 | tf_op jit(solution)/shard_map/ppermute | solution.py:13
  20.3 7.2 %collective-permute-start.2 = (f32[2,128,128]{2,1,0:T(8,128)S(1)}, f32[2,128,128]{2,1,0:T(8,128)S(1)}, u32[]{:S(2)}, u32[]{:S(2)}) collective-permute-start(f32[2,128,128]{2,1,0:T(8,128)S(1)} %slice.347), channel_id=1, source_target_pairs={{33,0},{34,1},{35,2},{36,3},{37,4},{38,5},{39,6},{40,7},{41,8},{42... | collective-permute-start | bytes 393224 | tf_op jit(solution)/shard_map/ppermute | solution.py:13
  93.3 2.1 copy-start.3
  95.4 1.2 copy-start.6
  96.6 2.0 copy-start.9
  235.9 16.6 %collective-permute-start.3 = (f32[3,128,256]{2,1,0:T(8,128)S(1)}, f32[3,128,256]{2,1,0:T(8,128)S(1)}, u32[]{:S(2)}, u32[]{:S(2)}) collective-permute-start(f32[3,128,256]{2,1,0:T(8,128)S(1)} %slice.359), channel_id=1, source_target_pairs={{0,32},{32,64},{64,96},{96,128},{128,160},{160,192},{192,224},{224... | collective-permute-start | bytes 1179656 | tf_op jit(solution)/shard_map/ppermute | solution.py:13
  247.9 9.9 %collective-permute-start.4 = (f32[3,256,128]{2,1,0:T(8,128)S(1)}, f32[3,256,128]{2,1,0:T(8,128)S(1)}, u32[]{:S(2)}, u32[]{:S(2)}) collective-permute-start(f32[3,256,128]{2,1,0:T(8,128)S(1)} %slice.361), channel_id=1, source_target_pairs={{0,1},{1,2},{2,3},{3,4},{4,5},{5,6},{6,7},{7,8},{8,9},{9,10},{10,1... | collective-permute-start | bytes 1179656 | tf_op jit(solution)/shard_map/ppermute | solution.py:13
  249.3 10.7 %copy-start.5 = (f32[2,256,256]{2,1,0:T(8,128)S(1)}, f32[2,256,256]{2,1,0:T(8,128)}, u32[]{:S(2)}) copy-start(f32[2,256,256]{2,1,0:T(8,128)} %param.29) | copy-start | bytes 1572868
  249.3 10.6 %collective-permute-start.5 = (f32[3,128,128]{2,1,0:T(8,128)S(1)}, f32[3,128,128]{2,1,0:T(8,128)S(1)}, u32[]{:S(2)}, u32[]{:S(2)}) collective-permute-start(f32[3,128,128]{2,1,0:T(8,128)S(1)} %slice.363), channel_id=1, source_target_pairs={{0,33},{1,34},{2,35},{3,36},{4,37},{5,38},{6,39},{7,40},{8,41},{9,... | collective-permute-start | bytes 589832 | tf_op jit(solution)/shard_map/ppermute | solution.py:13
  260.1 20.6 %collective-permute-start.6 = (f32[2,256,128]{2,1,0:T(8,128)S(1)}, f32[2,256,128]{2,1,0:T(8,128)S(1)}, u32[]{:S(2)}, u32[]{:S(2)}) collective-permute-start(f32[2,256,128]{2,1,0:T(8,128)S(1)} %slice.424), channel_id=1, source_target_pairs={{1,0},{2,1},{3,2},{4,3},{5,4},{6,5},{7,6},{8,7},{9,8},{10,9},{11,1... | collective-permute-start | bytes 786440 | tf_op jit(solution)/shard_map/ppermute | solution.py:13
  261.4 19.3 %collective-permute-start.7 = (f32[2,128,256]{2,1,0:T(8,128)S(1)}, f32[2,128,256]{2,1,0:T(8,128)S(1)}, u32[]{:S(2)}, u32[]{:S(2)}) collective-permute-start(f32[2,128,256]{2,1,0:T(8,128)S(1)} %slice.425), channel_id=1, source_target_pairs={{32,0},{64,32},{96,64},{128,96},{160,128},{192,160},{224,192},{256... | collective-permute-start | bytes 786440 | tf_op jit(solution)/shard_map/ppermute | solution.py:13
  263.3 17.3 %collective-permute-start.8 = (f32[2,128,128]{2,1,0:T(8,128)S(1)}, f32[2,128,128]{2,1,0:T(8,128)S(1)}, u32[]{:S(2)}, u32[]{:S(2)}) collective-permute-start(f32[2,128,128]{2,1,0:T(8,128)S(1)} %slice.426), channel_id=1, source_target_pairs={{33,0},{34,1},{35,2},{36,3},{37,4},{38,5},{39,6},{40,7},{41,8},{42... | collective-permute-start | bytes 393224 | tf_op jit(solution)/shard_map/ppermute | solution.py:13
  331.1 1.6 copy-start
  335.0 1.6 copy-start.2
  350.1 2.2 copy-start.1
  481.3 166.8 %copy-start.7 = (f32[2,128,128]{2,1,0:T(8,128)S(1)}, f32[2,128,128]{2,1,0:T(8,128)}, u32[]{:S(2)}) copy-start(f32[2,128,128]{2,1,0:T(8,128)} %param.30) | copy-start | bytes 393220
  482.2 167.6 %collective-permute-start.9 = (f32[2,128,256]{2,1,0:T(8,128)}, f32[2,128,256]{2,1,0:T(8,128)S(1)}, u32[]{:S(2)}, u32[]{:S(2)}) collective-permute-start(f32[2,128,256]{2,1,0:T(8,128)} %slice.375), channel_id=1, source_target_pairs={{0,32},{32,64},{64,96},{96,128},{128,160},{160,192},{192,224},{224... | collective-permute-start | bytes 786440 | tf_op jit(solution)/shard_map/ppermute | solution.py:13
  489.7 160.1 %collective-permute-start.10 = (f32[2,256,128]{2,1,0:T(8,128)S(1)}, f32[2,256,128]{2,1,0:T(8,128)}, u32[]{:S(2)}, u32[]{:S(2)}) collective-permute-start(f32[2,256,128]{2,1,0:T(8,128)S(1)} %slice.377), channel_id=1, source_target_pairs={{0,1},{1,2},{2,3},{3,4},{4,5},{5,6},{6,7},{7,8},{8,9},{9,10},{10,1... | collective-permute-start | bytes 786440 | tf_op jit(solution)/shard_map/ppermute | solution.py:13
  491.7 159.1 %collective-permute-start.11 = (f32[2,128,128]{2,1,0:T(8,128)S(1)}, f32[2,128,128]{2,1,0:T(8,128)S(1)}, u32[]{:S(2)}, u32[]{:S(2)}) collective-permute-start(f32[2,128,128]{2,1,0:T(8,128)S(1)} %slice.379), channel_id=1, source_target_pairs={{0,33},{1,34},{2,35},{3,36},{4,37},{5,38},{6,39},{7,40},{8,41},{9,... | collective-permute-start | bytes 393224 | tf_op jit(solution)/shard_map/ppermute | solution.py:13
Sparse Core Ops, SparseCore 0:
  354.1 291.8 all-reduce.1
where the time goes:
time: 664 us; the launch traced here: 659 us
  local copies, waits for them, and re-layouts  224 us (34%)
  waiting for transfers between devices  179 us (27%)
  loops' own time  132 us (20%)
  other arithmetic  63.8 us (10%)
  starting transfers between devices  41.5 us (6%)
  between operations  15.9 us (2%)
    psum x1, waiting for transfers between devices, on_device(): summed = lax.psum(gradient, ('row', 'col'))  153 us
    another operation x2, loops' own time, sweep(): deposit = lax.fori_loop(0, slots, place, deposit)  125 us
    gather x96, local copies, waits for them, and re-layouts  98 us
    dynamic_update_slice x32, local copies, waits for them, and re-layouts, place(): return lax.dynamic_update_slice(deposit, present + pushed[position], anchor)  83.9 us
    ppermute x12, starting transfers between devices, from_behind(): lax.ppermute(value, axis, [(source, source + steps) for source in range(f...  41.4 us
    add x32, other arithmetic, place(): return lax.dynamic_update_slice(deposit, present + pushed[position], anchor)  33.2 us
    ppermute x12, waiting for transfers between devices, from_behind(): lax.ppermute(value, axis, [(source, source + steps) for source in range(f...  25.5 us
    slice x32, local copies, waits for them, and re-layouts, place(): anchor = (zero_index, spot[0], spot[1])  18.3 us
  transfers between devices with their start and end apart: 13, of which 6 were waited for; matrix products, arithmetic and copies ran while one was open for 12% of the time, Pallas kernels for 0%

commit v1 on v0

--- a/solution.py
+++ b/solution.py
@@ -199,7 +199,7 @@
         False,
     )
     refined_object = updated + second_pass / denominator
-    summed = lax.psum(gradient, ("row", "col"))
+    summed = lax.psum(lax.psum(gradient, "col"), "row")
     spread = jnp.sqrt(jnp.mean(summed[0] * summed[0] + summed[1] * summed[1]) + 1e-06)
     new_probe = probe + summed / spread
     return (refined_object, new_probe)

time: 664 us -> 835 us (1.26)
  the two profiles are of different devices: /device:TPU:1 before, /device:TPU:43 now
where the time goes in v1:
time: 835 us; the launch traced here: 830 us
  waiting for transfers between devices  339 us (41%)
  local copies, waits for them, and re-layouts  224 us (27%)
  loops' own time  132 us (16%)
  other arithmetic  63.8 us (8%)
  starting transfers between devices  52 us (6%)
  between operations  15.9 us (2%)
    psum x2, waiting for transfers between devices, on_device(): summed = lax.psum(lax.psum(gradient, 'col'), 'row')  280 us
    another operation x2, loops' own time, sweep(): deposit = lax.fori_loop(0, slots, place, deposit)  126 us
    gather x96, local copies, waits for them, and re-layouts  98 us
    dynamic_update_slice x32, local copies, waits for them, and re-layouts, place(): return lax.dynamic_update_slice(deposit, present + pushed[position], anchor)  84.1 us
    ppermute x12, waiting for transfers between devices, from_behind(): lax.ppermute(value, axis, [(source, source + steps) for source in range(f...  59.2 us
    ppermute x12, starting transfers between devices, from_behind(): lax.ppermute(value, axis, [(source, source + steps) for source in range(f...  51.9 us
    add x32, other arithmetic, place(): return lax.dynamic_update_slice(deposit, present + pushed[position], anchor)  33.2 us
    slice x32, local copies, waits for them, and re-layouts, place(): anchor = (zero_index, spot[0], spot[1])  17.9 us
  transfers between devices with their start and end apart: 14, of which 8 were waited for; matrix products, arithmetic and copies ran while one was open for 9% of the time, Pallas kernels for 0%

profile of v1, /device:TPU:43, one launch (start us, length us, event | category | flops | bytes accessed | tf_op | source)
XLA Modules:
  0.0 830.3 jit_solution(5145954199344798090)
XLA Ops:
  8.2 11.3 %collective-permute-start = (f32[2,256,128]{2,1,0:T(8,128)S(1)}, f32[2,256,128]{2,1,0:T(8,128)S(1)}, u32[]{:S(2)}, u32[]{:S(2)}) collective-permute-start(f32[2,256,128]{2,1,0:T(8,128)S(1)} %slice.345), channel_id=1, source_target_pairs={{1,0},{2,1},{3,2},{4,3},{5,4},{6,5},{7,6},{8,7},{9,8},{10,9},{11,1... | collective-permute-start | bytes 786440 | tf_op jit(solution)/shard_map/ppermute | solution.py:13
  20.6 3.0 collective-permute-start.1
  35.1 49.5 %while.64 = (s32[]{:T(128)}, f32[2,384,384]{2,1,0:T(8,128)}, s32[16,3]{0,1:T(4,128)S(1)}, f32[16,2,128,128]{3,2,1,0:T(8,128)S(1)}, s32[]{:T(128)}) while((s32[]{:T(128)}, f32[2,384,384]{2,1,0:T(8,128)}, s32[16,3]{0,1:T(4,128)S(1)}, f32[16,2,128,128]{3,2,1,0:T(8,128)S(1)}, s32[]{:T(128)}) %tuple.206), condition=%wide.while_cond.6, body=%wide.while_body.6.sunk | while | flops 2 | bytes 262261 | solution.py:139
  35.8 2.4 bitcast_dynamic-update-slice_fusion.4
  38.9 2.4 bitcast_dynamic-update-slice_fusion.4
  42.0 2.4 bitcast_dynamic-update-slice_fusion.4
  45.1 2.4 bitcast_dynamic-update-slice_fusion.4
  48.1 2.4 bitcast_dynamic-update-slice_fusion.4
  51.2 2.4 bitcast_dynamic-update-slice_fusion.4
  54.3 2.4 bitcast_dynamic-update-slice_fusion.4
  57.4 2.4 bitcast_dynamic-update-slice_fusion.4
  60.5 2.4 bitcast_dynamic-update-slice_fusion.4
  63.6 2.4 bitcast_dynamic-update-slice_fusion.4
  66.7 2.4 bitcast_dynamic-update-slice_fusion.4
  69.8 2.4 bitcast_dynamic-update-slice_fusion.4
  72.9 2.4 bitcast_dynamic-update-slice_fusion.4
  76.0 2.4 bitcast_dynamic-update-slice_fusion.4
  79.1 2.4 bitcast_dynamic-update-slice_fusion.4
  82.2 2.4 bitcast_dynamic-update-slice_fusion.4
  87.3 12.3 %while.60 = (s32[]{:T(128)}, f32[16,2,128,128]{3,2,1,0:T(8,128)}, pred[16]{0:T(512)(128)(4,1)S(1)}, bf16[16,2,128,128]{2,3,1,0:T(8,128)(2,1)S(1)}, bf16[2,2,128,...) while((s32[]{:T(128)}, f32[16,2,128,128]{3,2,1,0:T(8,128)}, ...), condition=%wide.region_4.5_spmd, body=%wide.region_0.4_spmd.sunk | while | flops 269615104 | bytes 5898981 | solution.py:94
  104.8 137.4 %while.61 = (s32[]{:T(128)}, f32[3,384,384]{2,1,0:T(8,128)S(1)}, s32[16,2]{0,1:T(2,128)S(1)}, f32[16,3,128,128]{3,2,1,0:T(8,128)}, s32[]{:T(128)}, /*index=5*/s32[]{:T(128)}, s32[]{:T(128)}) while((s32[]{:T(128)}, f32[3,384,384]{2,1,0:T(8,128)S(1)}, s32[16,2]{0,1:T(2,128)S(1)}, f32[16,3,128,128]{3,2,1,0:T(8,128)}, s32[]{:T(128)}, ...), condition=%wide.region_6.7_spmd, body=%wide.region_5.6_spmd.sunk | while | flops 49160 | bytes 983237 | solution.py:162
  110.5 2.7 dynamic_update_slice.35
  118.9 3.0 dynamic_update_slice.35
  134.9 3.1 dynamic_update_slice.35
  143.6 3.0 dynamic_update_slice.35
  152.3 2.8 dynamic_update_slice.35
  160.8 2.8 dynamic_update_slice.35
  169.3 3.1 dynamic_update_slice.35
  178.1 3.1 dynamic_update_slice.35
  186.8 3.1 dynamic_update_slice.35
  195.6 3.0 dynamic_update_slice.35
  204.3 3.0 dynamic_update_slice.35
  213.0 3.1 dynamic_update_slice.35
  221.8 2.9 dynamic_update_slice.35
  230.4 3.1 dynamic_update_slice.35
  239.2 3.1 dynamic_update_slice.35
  242.3 3.6 collective-permute-start.3
  250.7 28.2 %collective-permute-done.4 = f32[3,256,128]{2,1,0:T(8,128)S(1)} collective-permute-done((f32[3,256,128]{2,1,0:T(8,128)S(1)}, f32[3,256,128]{2,1,0:T(8,128)S(1)}, u32[]{:S(2)}, u32[]{:S(2)}) %collective-permute-start.4) | collective-permute-done | bytes 393248 | tf_op jit(solution)/shard_map/ppermute | solution.py:13
  279.0 4.7 collective-permute-done.5
  285.8 2.9 collective-permute-start.7
  290.7 7.7 collective-permute-done.8
  299.7 49.1 %while.65 = (s32[]{:T(128)}, f32[2,384,384]{2,1,0:T(8,128)}, s32[16,3]{0,1:T(4,128)S(1)}, f32[16,2,128,128]{3,2,1,0:T(8,128)S(1)}, s32[]{:T(128)}) while((s32[]{:T(128)}, f32[2,384,384]{2,1,0:T(8,128)}, s32[16,3]{0,1:T(4,128)S(1)}, f32[16,2,128,128]{3,2,1,0:T(8,128)S(1)}, s32[]{:T(128)}) %tuple.237), condition=%wide.while_cond.7, body=%wide.while_body.7.sunk | while | flops 2 | bytes 262261 | solution.py:139
  303.5 2.4 bitcast_dynamic-update-slice_fusion.5
  309.6 2.4 bitcast_dynamic-update-slice_fusion.5
  312.7 2.4 bitcast_dynamic-update-slice_fusion.5
  315.7 2.4 bitcast_dynamic-update-slice_fusion.5
  318.8 2.4 bitcast_dynamic-update-slice_fusion.5
  324.9 2.4 bitcast_dynamic-update-slice_fusion.5
  354.3 13.6 %while.62 = (s32[]{:T(128)}, f32[16,2,128,128]{3,2,1,0:T(8,128)}, pred[16]{0:T(512)(128)(4,1)S(1)}, bf16[16,2,128,128]{2,3,1,0:T(8,128)(2,1)S(1)}, bf16[2,2,128,...) while((s32[]{:T(128)}, f32[16,2,128,128]{3,2,1,0:T(8,128)}, ...), condition=%wide.region_11.12_spmd, body=%wide.region_7.11_spmd.sunk | while | flops 269615104 | bytes 5898981 | solution.py:94
  373.3 279.8 %all-reduce.3.cloned.1.call-done = f32[2,128,128]{2,1,0:T(8,128)} async-done(((f32[2,128,128]{2,1,0:T(8,128)}), f32[2,128,128]{2,1,0:T(8,128)}) %all-reduce.3.cloned.1.call-update) | async-done | bytes 131088 | tf_op jit(solution)/shard_map/psum | solution.py:202
  653.2 126.3 %while.63 = (s32[]{:T(128)}, f32[2,384,384]{2,1,0:T(8,128)S(1)}, s32[16,2]{0,1:T(2,128)S(1)}, f32[16,2,128,128]{3,2,1,0:T(8,128)}, s32[]{:T(128)}, /*index=5*/s32[]{:T(128)}, s32[]{:T(128)}) while((s32[]{:T(128)}, f32[2,384,384]{2,1,0:T(8,128)S(1)}, s32[16,2]{0,1:T(2,128)S(1)}, f32[16,2,128,128]{3,2,1,0:T(8,128)}, s32[]{:T(128)}, ...), condition=%wide.region_13.14_spmd, body=%wide.region_12.13_spmd.sunk | while | flops 32776 | bytes 655557 | solution.py:162
  666.3 2.5 dynamic_update_slice.37
  681.3 2.5 dynamic_update_slice.37
  689.4 2.4 dynamic_update_slice.37
  712.9 2.5 dynamic_update_slice.37
  720.9 2.5 dynamic_update_slice.37
  728.9 2.5 dynamic_update_slice.37
  737.0 2.5 dynamic_update_slice.37
  745.0 2.5 dynamic_update_slice.37
  753.0 2.5 dynamic_update_slice.37
  768.9 2.5 dynamic_update_slice.37
  776.9 2.5 dynamic_update_slice.37
  780.3 17.4 %collective-permute-start.9 = (f32[2,128,256]{2,1,0:T(8,128)}, f32[2,128,256]{2,1,0:T(8,128)S(1)}, u32[]{:S(2)}, u32[]{:S(2)}) collective-permute-start(f32[2,128,256]{2,1,0:T(8,128)} %slice.375), channel_id=1, source_target_pairs={{0,32},{32,64},{64,96},{96,128},{128,160},{160,192},{192,224},{224... | collective-permute-start | bytes 786440 | tf_op jit(solution)/shard_map/ppermute | solution.py:13
  805.3 14.8 %collective-permute-done.10 = f32[2,256,128]{2,1,0:T(8,128)} collective-permute-done((f32[2,256,128]{2,1,0:T(8,128)S(1)}, f32[2,256,128]{2,1,0:T(8,128)}, u32[]{:S(2)}, u32[]{:S(2)}) %collective-permute-start.10) | collective-permute-done | bytes 262176 | tf_op jit(solution)/shard_map/ppermute | solution.py:13
  (324 shorter events, 190.3 us)
Async XLA Ops:
  7.2 24.4 %copy-start.8 = (bf16[1,1,16,128,128]{4,3,2,1,0:T(8,128)(2,1)S(1)}, bf16[1,1,16,128,128]{4,3,2,1,0:T(8,128)(2,1)}, u32[]{:S(2)}) copy-start(bf16[1,1,16,128,128]{4,3,2,1,0:T(8,128)(2,1)} %param.31) | copy-start | bytes 1572868
  7.2 645.9 %all-reduce.3.cloned.1.call-start = ((), (), s32[]{:S(2)}) async-start(), calls=%async_computation | async-start | bytes 262144 | tf_op jit(solution)/shard_map/psum | solution.py:202
  8.2 25.5 %collective-permute-start = (f32[2,256,128]{2,1,0:T(8,128)S(1)}, f32[2,256,128]{2,1,0:T(8,128)S(1)}, u32[]{:S(2)}, u32[]{:S(2)}) collective-permute-start(f32[2,256,128]{2,1,0:T(8,128)S(1)} %slice.345), channel_id=1, source_target_pairs={{1,0},{2,1},{3,2},{4,3},{5,4},{6,5},{7,6},{8,7},{9,8},{10,9},{11,1... | collective-permute-start | bytes 786440 | tf_op jit(solution)/shard_map/ppermute | solution.py:13
  20.6 13.2 %copy-start.4 = (f32[2,256,256]{2,1,0:T(8,128)S(1)}, f32[2,256,256]{2,1,0:T(8,128)}, u32[]{:S(2)}) copy-start(f32[2,256,256]{2,1,0:T(8,128)} %param.29) | copy-start | bytes 1572868
  20.6 13.2 %collective-permute-start.1 = (f32[2,128,256]{2,1,0:T(8,128)S(1)}, f32[2,128,256]{2,1,0:T(8,128)S(1)}, u32[]{:S(2)}, u32[]{:S(2)}) collective-permute-start(f32[2,128,256]{2,1,0:T(8,128)S(1)} %slice.346), channel_id=1, source_target_pairs={{32,0},{64,32},{96,64},{128,96},{160,128},{192,160},{224,192},{256... | collective-permute-start | bytes 786440 | tf_op jit(solution)/shard_map/ppermute | solution.py:13
  24.5 9.2 %collective-permute-start.2 = (f32[2,128,128]{2,1,0:T(8,128)S(1)}, f32[2,128,128]{2,1,0:T(8,128)S(1)}, u32[]{:S(2)}, u32[]{:S(2)}) collective-permute-start(f32[2,128,128]{2,1,0:T(8,128)S(1)} %slice.347), channel_id=1, source_target_pairs={{33,0},{34,1},{35,2},{36,3},{37,4},{38,5},{39,6},{40,7},{41,8},{42... | collective-permute-start | bytes 393224 | tf_op jit(solution)/shard_map/ppermute | solution.py:13
  99.5 2.1 copy-start.3
  101.6 1.2 copy-start.6
  102.8 2.0 copy-start.9
  242.3 8.3 %collective-permute-start.3 = (f32[3,128,256]{2,1,0:T(8,128)S(1)}, f32[3,128,256]{2,1,0:T(8,128)S(1)}, u32[]{:S(2)}, u32[]{:S(2)}) collective-permute-start(f32[3,128,256]{2,1,0:T(8,128)S(1)} %slice.359), channel_id=1, source_target_pairs={{0,32},{32,64},{64,96},{96,128},{128,160},{160,192},{192,224},{224... | collective-permute-start | bytes 1179656 | tf_op jit(solution)/shard_map/ppermute | solution.py:13
  245.9 32.9 %collective-permute-start.4 = (f32[3,256,128]{2,1,0:T(8,128)S(1)}, f32[3,256,128]{2,1,0:T(8,128)S(1)}, u32[]{:S(2)}, u32[]{:S(2)}) collective-permute-start(f32[3,256,128]{2,1,0:T(8,128)S(1)} %slice.361), channel_id=1, source_target_pairs={{0,1},{1,2},{2,3},{3,4},{4,5},{5,6},{6,7},{7,8},{8,9},{9,10},{10,1... | collective-permute-start | bytes 1179656 | tf_op jit(solution)/shard_map/ppermute | solution.py:13
  247.9 35.8 %copy-start.5 = (f32[2,256,256]{2,1,0:T(8,128)S(1)}, f32[2,256,256]{2,1,0:T(8,128)}, u32[]{:S(2)}) copy-start(f32[2,256,256]{2,1,0:T(8,128)} %param.29) | copy-start | bytes 1572868
  248.0 35.7 %collective-permute-start.5 = (f32[3,128,128]{2,1,0:T(8,128)S(1)}, f32[3,128,128]{2,1,0:T(8,128)S(1)}, u32[]{:S(2)}, u32[]{:S(2)}) collective-permute-start(f32[3,128,128]{2,1,0:T(8,128)S(1)} %slice.363), channel_id=1, source_target_pairs={{0,33},{1,34},{2,35},{3,36},{4,37},{5,38},{6,39},{7,40},{8,41},{9,... | collective-permute-start | bytes 589832 | tf_op jit(solution)/shard_map/ppermute | solution.py:13
  283.9 14.5 %collective-permute-start.6 = (f32[2,256,128]{2,1,0:T(8,128)S(1)}, f32[2,256,128]{2,1,0:T(8,128)S(1)}, u32[]{:S(2)}, u32[]{:S(2)}) collective-permute-start(f32[2,256,128]{2,1,0:T(8,128)S(1)} %slice.424), channel_id=1, source_target_pairs={{1,0},{2,1},{3,2},{4,3},{5,4},{6,5},{7,6},{8,7},{9,8},{10,9},{11,1... | collective-permute-start | bytes 786440 | tf_op jit(solution)/shard_map/ppermute | solution.py:13
  285.8 12.5 %collective-permute-start.7 = (f32[2,128,256]{2,1,0:T(8,128)S(1)}, f32[2,128,256]{2,1,0:T(8,128)S(1)}, u32[]{:S(2)}, u32[]{:S(2)}) collective-permute-start(f32[2,128,256]{2,1,0:T(8,128)S(1)} %slice.425), channel_id=1, source_target_pairs={{32,0},{64,32},{96,64},{128,96},{160,128},{192,160},{224,192},{256... | collective-permute-start | bytes 786440 | tf_op jit(solution)/shard_map/ppermute | solution.py:13
  288.7 9.6 %collective-permute-start.8 = (f32[2,128,128]{2,1,0:T(8,128)S(1)}, f32[2,128,128]{2,1,0:T(8,128)S(1)}, u32[]{:S(2)}, u32[]{:S(2)}) collective-permute-start(f32[2,128,128]{2,1,0:T(8,128)S(1)} %slice.426), channel_id=1, source_target_pairs={{33,0},{34,1},{35,2},{36,3},{37,4},{38,5},{39,6},{40,7},{41,8},{42... | collective-permute-start | bytes 393224 | tf_op jit(solution)/shard_map/ppermute | solution.py:13
  348.8 1.6 copy-start
  352.7 1.6 copy-start.2
  367.9 2.2 copy-start.1
  371.7 429.8 %all-reduce.5.cloned.1.call-start = ((), (), s32[]{:S(2)}) async-start(), calls=%async_computation.1 | async-start | bytes 262144 | tf_op jit(solution)/shard_map/psum | solution.py:202
  779.4 24.3 %copy-start.7 = (f32[2,128,128]{2,1,0:T(8,128)S(1)}, f32[2,128,128]{2,1,0:T(8,128)}, u32[]{:S(2)}) copy-start(f32[2,128,128]{2,1,0:T(8,128)} %param.30) | copy-start | bytes 393220
  780.3 25.0 %collective-permute-start.9 = (f32[2,128,256]{2,1,0:T(8,128)}, f32[2,128,256]{2,1,0:T(8,128)S(1)}, u32[]{:S(2)}, u32[]{:S(2)}) collective-permute-start(f32[2,128,256]{2,1,0:T(8,128)} %slice.375), channel_id=1, source_target_pairs={{0,32},{32,64},{64,96},{96,128},{128,160},{160,192},{192,224},{224... | collective-permute-start | bytes 786440 | tf_op jit(solution)/shard_map/ppermute | solution.py:13
  797.6 22.5 %collective-permute-start.10 = (f32[2,256,128]{2,1,0:T(8,128)S(1)}, f32[2,256,128]{2,1,0:T(8,128)}, u32[]{:S(2)}, u32[]{:S(2)}) collective-permute-start(f32[2,256,128]{2,1,0:T(8,128)S(1)} %slice.377), channel_id=1, source_target_pairs={{0,1},{1,2},{2,3},{3,4},{4,5},{5,6},{6,7},{7,8},{8,9},{9,10},{10,1... | collective-permute-start | bytes 786440 | tf_op jit(solution)/shard_map/ppermute | solution.py:13
  799.6 23.0 %collective-permute-start.11 = (f32[2,128,128]{2,1,0:T(8,128)S(1)}, f32[2,128,128]{2,1,0:T(8,128)S(1)}, u32[]{:S(2)}, u32[]{:S(2)}) collective-permute-start(f32[2,128,128]{2,1,0:T(8,128)S(1)} %slice.379), channel_id=1, source_target_pairs={{0,33},{1,34},{2,35},{3,36},{4,37},{5,38},{6,39},{7,40},{8,41},{9,... | collective-permute-start | bytes 393224 | tf_op jit(solution)/shard_map/ppermute | solution.py:13
Sparse Core Ops, SparseCore 0:
  371.9 281.1 all-reduce.2
  655.9 134.7 all-reduce.4
